TPU v7x, 32 devices: a whole 2x2x4 slice. The times are simulated.
32 devices in a mesh: row: 8 (over z, x), col: 4 (over y, core).
Axes of the slice: x: 2, y: 2, z: 4, core: 2. Of those that a mesh axis runs over, the one named last changes fastest.
Arguments:
- gradients: bfloat16 [32, 1024, 5120], P(('row', 'col')), may hold values from -24 to 24
- bucket_lengths: int32 [16], replicated, may hold values from 1 to 128, 1024 in all
- owner_offset: int32 [8], replicated, may hold values from 0 to 3
- clip_rms: float32 [1], replicated, may hold values from 0.15 to 0.4
Outputs:
- clipped_shard: float32 [1024, 5120], P('row', 'col')
- bucket_rms: float32 [16], replicated
Inputs may be any that keep to these rules, and one draw needn't show every extreme that they name: `bucket_lengths`: the buckets cover all 1024 rows; the largest has exactly 128 rows.
All inputs are finite; a program needn't handle non-finite values.
Results may differ from a plain program's by a relative error of at most 0.0003.
Values sent between devices are 32-bit elements; how exact they have to be, the bound alone decides.
A program may use at most 128 MiB of HBM per device.

v0:
```python
import jax
import jax.numpy as jnp
from jax import lax
from jax.sharding import PartitionSpec as P


def turn_block(block, shift):
    return jnp.roll(block, -shift, axis=1)


def shards(gradients, bucket_lengths, owner_offset, clip_rms):
    n_row = lax.axis_size("row")
    n_col = lax.axis_size("col")
    devices = n_row * n_col
    source = gradients[0]
    total_rows, width = source.shape
    width_local = width // n_col
    rows_local = total_rows // n_row
    row_index = lax.axis_index("row")
    blocks = source.reshape(n_row, rows_local, n_col, width_local)
    blocks = jax.vmap(turn_block)(blocks, owner_offset)
    blocks = (
        blocks.transpose(0, 2, 1, 3).reshape(devices * rows_local, width_local).astype(jnp.float32)
    )
    summed = lax.psum_scatter(blocks, ("row", "col"), scatter_dimension=0, tiled=True)
    averaged = summed / devices
    ends = jnp.cumsum(bucket_lengths)
    starts = ends - bucket_lengths
    row_ids = row_index * rows_local + jnp.arange(rows_local, dtype=jnp.int32)
    member = ((row_ids[:, None] >= starts[None, :]) & (row_ids[:, None] < ends[None, :])).astype(
        jnp.float32
    )
    row_squares = jnp.sum(averaged * averaged, axis=1)
    local_squares = jnp.sum(row_squares[:, None] * member, axis=0)
    bucket_squares = lax.psum(local_squares, ("row", "col"))
    overall = jnp.sqrt(jnp.sum(bucket_squares) / (total_rows * width))
    factor = clip_rms[0] / jnp.maximum(overall, clip_rms[0])
    clipped_shard = averaged * factor
    bucket_rms = jnp.sqrt(bucket_squares / (bucket_lengths.astype(jnp.float32) * width))
    return (clipped_shard, bucket_rms)


def solution(mesh):
    in_specs = (P(("row", "col"), None, None), P(), P(), P())
    out_specs = (P("row", "col"), P())
    return jax.shard_map(shards, mesh=mesh, in_specs=in_specs, out_specs=out_specs, check_vma=False)
```

profile of v0, /device:TPU:0, one launch (start us, length us, event | category | flops | bytes accessed | tf_op | source)
XLA Modules:
  0.0 363.9 jit_solution(11172365279284914420)
XLA Ops:
  7.2 0.0 reduce-scatter.2.cloned.1.call-start
  7.2 19.4 %reshape.50 = bf16[8,128,4,1280]{3,2,1,0:T(4,128)(2,1)} reshape(bf16[1,1024,5120]{2,1,0:T(8,128)(2,1)} %param.4) | data formatting | bytes 20971520 | tf_op jit(solution)/shard_map/reshape;squeeze | solution.py:20
  26.6 9.8 %copy.12 = bf16[8,128,4,1280]{3,1,0,2:T(8,128)(2,1)} copy(bf16[8,128,4,1280]{3,2,1,0:T(4,128)(2,1)} %reshape.50) | data formatting | bytes 20971520 | tf_op jit(solution)/shard_map/reshape;squeeze | solution.py:20
  36.4 0.0 copy-start.1
  36.4 17.5 %pad_maximum_fusion = bf16[8,128,8,1280]{3,1,0,2:T(8,128)(2,1)} fusion(bf16[8,128,4,1280]{3,1,0,2:T(8,128)(2,1)} %copy.12), kind=kLoop, calls=%fused_computation.1 | loop fusion | flops 10485760 | bytes 31457280 | tf_op jit(solution)/shard_map/vmap(jit(_roll_dynamic))/concatenate | solution.py:8
  53.9 0.0 copy-done.1
  54.0 12.7 %gather_fusion = bf16[8,128,4,1280]{3,1,2,0:T(8,128)(2,1)} fusion(bf16[8,128,8,1280]{3,1,0,2:T(8,128)(2,1)} %pad_maximum_fusion, s32[8]{0:T(128)S(1)} %fusion.2), kind=kCustom, calls=%fused_computation | custom fusion | bytes 20971648 | tf_op jit(solution)/shard_map/vmap(jit(_roll_dynamic))/gather | solution.py:8
  66.6 13.6 %convert_element_type.18 = f32[8,128,4,1280]{3,1,2,0:T(8,128)} convert(bf16[8,128,4,1280]{3,1,2,0:T(8,128)(2,1)} %gather_fusion) | non-fusion elementwise | flops 5242880 | bytes 31457280 | tf_op jit(solution)/shard_map/convert_element_type | solution.py:23
  80.2 0.0 copy-start
  80.2 0.0 reduce-scatter.2.cloned.1.call-update
  80.3 0.6 copy-done
  80.9 0.1 copy.14
  81.0 0.1 reduce
  81.1 227.2 %reduce-scatter.2.cloned.1.call-done = f32[128,1280]{1,0:T(8,128)} async-done(((f32[4096,1280]{1,0:T(8,128)}), f32[128,1280]{1,0:T(8,128)}) %reduce-scatter.2.cloned.1.call-update) | async-done | bytes 655376 | tf_op jit(solution)/shard_map/reduce_scatter | solution.py:25
  308.3 1.2 multiply_reduce_fusion
  309.6 0.2 select_reduce_fusion
  310.4 42.7 %psum.7 = f32[16]{0:T(128)S(1)} all-reduce(f32[16]{0:T(128)S(1)} %select_reduce_fusion), channel_id=1, replica_groups=mesh['row'=8,'col'=4] {'row','col'}, use_global_device_ids=true, to_apply=%region_4.5 | all-reduce | flops 16 | bytes 128 | tf_op jit(solution)/shard_map/psum | solution.py:35
  353.1 1.2 fusion.3
  355.1 2.0 broadcast_multiply_fusion
  (4 shorter events, 0.1 us)
Async XLA Ops:
  7.2 301.2 %reduce-scatter.2.cloned.1.call-start = ((), (), s32[]{:S(2)}) async-start(), calls=%async_computation.1 | async-start | bytes 21626880 | tf_op jit(solution)/shard_map/reduce_scatter | solution.py:25
  36.4 17.5 %copy-start.1 = (s32[8]{0:T(128)S(1)}, s32[8]{0:T(128)}, u32[]{:S(2)}) copy-start(s32[8]{0:T(128)} %param.6) | copy-start | bytes 100
  80.2 0.7 copy-start
Sparse Core Ops, SparseCore 0:
  80.4 227.9 reduce-scatter.1
where the time goes:
time: 365 us; the launch traced here: 364 us
  waiting for transfers between devices  227 us (62%)
  blocking collectives  42.7 us (12%)
  local copies, waits for them, and re-layouts  42.6 us (12%)
  other arithmetic  35.9 us (10%)
  between operations  15.5 us (4%)
    reduce_scatter x1, waiting for transfers between devices, shards(): lax.psum_scatter(blocks, ('row', 'col'), scatter_dimension=0, tiled=True)  227 us
    psum x1, blocking collectives, shards(): bucket_squares = lax.psum(local_squares, ('row', 'col'))  42.7 us
    another operation x2, local copies, waits for them, and re-layouts, shards(): blocks = source.reshape(n_row, rows_local, n_col, width_local)  29.2 us
    concatenate x1, other arithmetic, turn_block(): return jnp.roll(block, -shift, axis=1)  17.5 us
    convert_element_type x1, other arithmetic, shards(): blocks.transpose(0, 2, 1, 3).reshape(devices * rows_local, width_local)  13.6 us
    gather x1, local copies, waits for them, and re-layouts, turn_block(): return jnp.roll(block, -shift, axis=1)  12.7 us
  transfers between devices with their start and end apart: 1, of which 1 were waited for; matrix products, arithmetic and copies ran while one was open for 0% of the time, Pallas kernels for 0%

commit v1 on v0

--- a/solution.py
+++ b/solution.py
@@ -2,6 +2,8 @@
 import jax.numpy as jnp
 from jax import lax
 from jax.sharding import PartitionSpec as P
+
+number_levels_all = lambda s0, which_axis, axis_key: lax.psum(lax.psum(s0, axis_key), which_axis)
 
 
 def turn_block(block, shift):
@@ -32,7 +34,7 @@
     )
     row_squares = jnp.sum(averaged * averaged, axis=1)
     local_squares = jnp.sum(row_squares[:, None] * member, axis=0)
-    bucket_squares = lax.psum(local_squares, ("row", "col"))
+    bucket_squares = number_levels_all(local_squares, "row", "col")
     overall = jnp.sqrt(jnp.sum(bucket_squares) / (total_rows * width))
     factor = clip_rms[0] / jnp.maximum(overall, clip_rms[0])
     clipped_shard = averaged * factor

time: 365 us -> 351 us (0.962)
  blocking collectives: 42.7 us -> 29.2 us
    psum x1 -> x2, blocking collectives: 42.7 us -> 29.2 us  [the longest x1 21.1 us: lax.psum(lax.psum(s0, axis_key), which_axis)]
where the time goes in v1:
time: 351 us; the launch traced here: 350 us
  waiting for transfers between devices  227 us (65%)
  local copies, waits for them, and re-layouts  42.6 us (12%)
  other arithmetic  35.9 us (10%)
  blocking collectives  29.2 us (8%)
  between operations  15.5 us (4%)
    reduce_scatter x1, waiting for transfers between devices, shards(): lax.psum_scatter(blocks, ('row', 'col'), scatter_dimension=0, tiled=True)  227 us
    another operation x2, local copies, waits for them, and re-layouts, shards(): blocks = source.reshape(n_row, rows_local, n_col, width_local)  29.2 us
    psum x1, blocking collectives, lax.psum(lax.psum(s0, axis_key), which_axis)  21.1 us
    concatenate x1, other arithmetic, turn_block(): return jnp.roll(block, -shift, axis=1)  17.5 us
    convert_element_type x1, other arithmetic, shards(): blocks.transpose(0, 2, 1, 3).reshape(devices * rows_local, width_local)  13.6 us
    gather x1, local copies, waits for them, and re-layouts, turn_block(): return jnp.roll(block, -shift, axis=1)  12.7 us
    psum x1, blocking collectives, lax.psum(s0, axis_key)  8.14 us
  transfers between devices with their start and end apart: 1, of which 1 were waited for; matrix products, arithmetic and copies ran while one was open for 0% of the time, Pallas kernels for 0%

profile of v1, /device:TPU:0, one launch (start us, length us, event | category | flops | bytes accessed | tf_op | source)
XLA Modules:
  0.0 350.4 jit_solution(12839309980723878688)
XLA Ops:
  7.2 0.0 reduce-scatter.2.cloned.1.call-start
  7.2 19.4 %reshape.50 = bf16[8,128,4,1280]{3,2,1,0:T(4,128)(2,1)} reshape(bf16[1,1024,5120]{2,1,0:T(8,128)(2,1)} %param.4) | data formatting | bytes 20971520 | tf_op jit(solution)/shard_map/reshape;squeeze | solution.py:22
  26.6 9.8 %copy.12 = bf16[8,128,4,1280]{3,1,0,2:T(8,128)(2,1)} copy(bf16[8,128,4,1280]{3,2,1,0:T(4,128)(2,1)} %reshape.50) | data formatting | bytes 20971520 | tf_op jit(solution)/shard_map/reshape;squeeze | solution.py:22
  36.4 0.0 copy-start.1
  36.4 17.5 %pad_maximum_fusion = bf16[8,128,8,1280]{3,1,0,2:T(8,128)(2,1)} fusion(bf16[8,128,4,1280]{3,1,0,2:T(8,128)(2,1)} %copy.12), kind=kLoop, calls=%fused_computation.1 | loop fusion | flops 10485760 | bytes 31457280 | tf_op jit(solution)/shard_map/vmap(jit(_roll_dynamic))/concatenate | solution.py:10
  53.9 0.0 copy-done.1
  54.0 12.7 %gather_fusion = bf16[8,128,4,1280]{3,1,2,0:T(8,128)(2,1)} fusion(bf16[8,128,8,1280]{3,1,0,2:T(8,128)(2,1)} %pad_maximum_fusion, s32[8]{0:T(128)S(1)} %fusion.2), kind=kCustom, calls=%fused_computation | custom fusion | bytes 20971648 | tf_op jit(solution)/shard_map/vmap(jit(_roll_dynamic))/gather | solution.py:10
  66.6 13.6 %convert_element_type.18 = f32[8,128,4,1280]{3,1,2,0:T(8,128)} convert(bf16[8,128,4,1280]{3,1,2,0:T(8,128)(2,1)} %gather_fusion) | non-fusion elementwise | flops 5242880 | bytes 31457280 | tf_op jit(solution)/shard_map/convert_element_type | solution.py:25
  80.2 0.0 copy-start
  80.2 0.0 reduce-scatter.2.cloned.1.call-update
  80.3 0.6 copy-done
  80.9 0.1 copy.14
  81.0 0.1 reduce
  81.1 227.2 %reduce-scatter.2.cloned.1.call-done = f32[128,1280]{1,0:T(8,128)} async-done(((f32[4096,1280]{1,0:T(8,128)}), f32[128,1280]{1,0:T(8,128)}) %reduce-scatter.2.cloned.1.call-update) | async-done | bytes 655376 | tf_op jit(solution)/shard_map/reduce_scatter | solution.py:27
  308.3 1.2 multiply_reduce_fusion
  309.6 0.2 select_reduce_fusion
  309.7 8.1 %psum.14 = f32[16]{0:T(128)S(1)} all-reduce(f32[16]{0:T(128)S(1)} %select_reduce_fusion), channel_id=1, replica_groups=mesh['row'=8,'col'=4] {'col'}, use_global_device_ids=true, to_apply=%region_4.5 | all-reduce | flops 16 | bytes 128 | tf_op jit(solution)/shard_map/psum | solution.py:6
  318.5 21.1 %psum.15 = f32[16]{0:T(128)S(1)} all-reduce(f32[16]{0:T(128)S(1)} %psum.14), channel_id=1, replica_groups=mesh['row'=8,'col'=4] {'row'}, use_global_device_ids=true, to_apply=%region_5.6 | all-reduce | flops 16 | bytes 128 | tf_op jit(solution)/shard_map/psum | solution.py:6
  339.6 1.2 fusion.3
  341.6 2.0 broadcast_multiply_fusion
  (4 shorter events, 0.1 us)
Async XLA Ops:
  7.2 301.2 %reduce-scatter.2.cloned.1.call-start = ((), (), s32[]{:S(2)}) async-start(), calls=%async_computation.1 | async-start | bytes 21626880 | tf_op jit(solution)/shard_map/reduce_scatter | solution.py:27
  36.4 17.5 %copy-start.1 = (s32[8]{0:T(128)S(1)}, s32[8]{0:T(128)}, u32[]{:S(2)}) copy-start(s32[8]{0:T(128)} %param.6) | copy-start | bytes 100
  80.2 0.7 copy-start
Sparse Core Ops, SparseCore 0:
  80.4 227.9 reduce-scatter.1
